TPU v7x, 32 devices: a whole 2x2x4 slice. The times are simulated.
32 devices in a mesh: dp: 2 (over x), row: 4 (over y, core), col: 4 (over z).
Axes of the slice: x: 2, y: 2, z: 4, core: 2. Of those that a mesh axis runs over, the one named last changes fastest.
Arguments:
- inputs: bfloat16 [4096, 2048], P(('dp', 'row'), 'col'), may hold values from -6 to 6
- cotangent: bfloat16 [4096, 2048], P(('dp', 'row'), 'col'), may hold values from -6 to 6
- segments: int32 [4096], P('dp'), may hold values from 1999 to 4095, as said below
- positions: int32 [4096], P('dp'), may hold values from 0 to 1999, as said below
- w_qkv: bfloat16 [2048, 3, 2048], P('col', None, 'row'), may hold values from -1 to 1
- w_out: bfloat16 [2048, 2048], P('row', 'col'), may hold values from -0.5 to 0.5
- w_up: bfloat16 [2048, 8192], P('col', 'row'), may hold values from -1 to 1
- w_down: bfloat16 [8192, 2048], P('row', 'col'), may hold values from -0.0625 to 0.0625
- vectors: float32 [11, 2048], replicated, may hold values from -1.5 to 3
- tile_moment: float32 [4, 4, 24, 512, 256], P('row', 'col', 'dp'), may hold values from -40 to 40
- vector_moment: float32 [11, 2048], replicated, may hold values from -3 to 3
Outputs:
- result: float32 [4096, 2048], P(('dp', 'row'), 'col')
- grad_input: float32 [4096, 2048], P(('dp', 'row'), 'col')
- tile_grads: float32 [4, 4, 24, 512, 256], P('row', 'col', 'dp')
- new_tiles: float32 [4, 4, 24, 512, 256], P('row', 'col', 'dp')
- new_tile_moment: float32 [4, 4, 24, 512, 256], P('row', 'col', 'dp')
- vector_grads: float32 [11, 2048], replicated
- new_vectors: float32 [11, 2048], replicated
- new_vector_moment: float32 [11, 2048], replicated
Inputs may be any that keep to these rules, and one draw needn't show every extreme that they name: `segments`: each token's document label, the index in the whole array of its document's last token (the last document's label is 4095); labels never fall; every document but the last has 200 to 2000 tokens, documents run on across sequence ends, and the first has exactly 2000. `positions`: each token's place in its document, counted from 0 and running on across sequence ends.
All inputs are finite; a program needn't handle non-finite values.
Results may differ from a plain program's by a relative error of at most 0.015.
The roundings to bfloat16 on the way count: a program that leaves them out, or rounds other values in their place, can miss the bound.
Values may be sent and summed in bfloat16 or wider, within the bound.
A program may use at most 256 MiB of HBM per device.

v0:
```python
import math
import jax
import jax.numpy as jnp
from jax import lax
from jax.sharding import PartitionSpec as P

HEAD_DIM = 64
ROTARY = 32
SEQ_LEN = 512
MOMENTUM_RATE = 0.95
MUON_RATE = 0.05
VECTOR_RATE = 0.12
NEWTON_A = 3.4445
NEWTON_B = -4.775
NEWTON_C = 2.0315
GELU_SCALE = 0.7978845608028654
GELU_CUBIC = 0.044715
NORM_EPS = 1e-05
STAT_EPS = 1e-06
MASKED_SCORE = -1e30


def to_low(tensor_in):
    return lax.optimization_barrier(tensor_in.astype(jnp.bfloat16))


def gelu_value(pre_act):
    inner_arg = GELU_SCALE * (pre_act + GELU_CUBIC * pre_act * pre_act * pre_act)
    return 0.5 * pre_act * (1.0 + jnp.tanh(inner_arg))


def gelu_slope(pre_act):
    tanh_val = jnp.tanh(GELU_SCALE * (pre_act + GELU_CUBIC * pre_act * pre_act * pre_act))
    return 0.5 * (1.0 + tanh_val) + 0.5 * pre_act * (1.0 - tanh_val * tanh_val) * GELU_SCALE * (
        1.0 + 3.0 * GELU_CUBIC * pre_act * pre_act
    )


def rotary_tables(positions):
    half_dims = ROTARY // 2
    frequency = jnp.exp(
        jnp.arange(half_dims, dtype=jnp.float32) * (-2.0 * math.log(10000.0) / ROTARY)
    )
    angles = positions.astype(jnp.float32)[:, None] * frequency[None, :]
    return (jnp.cos(angles), jnp.sin(angles))


def rotate(tensor_in, cosine, sine_tab, direction_sign):
    half_dims = ROTARY // 2
    first_half = tensor_in[..., :half_dims]
    second_half = tensor_in[..., half_dims:ROTARY]
    cos_wide = cosine[:, None, :]
    sin_wide = sine_tab[:, None, :] * direction_sign
    return jnp.concatenate(
        [
            first_half * cos_wide - second_half * sin_wide,
            second_half * cos_wide + first_half * sin_wide,
            tensor_in[..., ROTARY:],
        ],
        axis=-1,
    )


def causal_allowed(segment):
    token_order = jnp.arange(segment.shape[0])
    return (segment[:, None] == segment[None, :]) & (token_order[:, None] >= token_order[None, :])


def masked_scores(queries, key_vecs, segment, score_scale):
    scores = (
        jnp.einsum("lhe,mhe->hlm", queries, key_vecs, preferred_element_type=jnp.float32)
        * score_scale
    )
    return jnp.where(causal_allowed(segment)[None], scores, MASKED_SCORE)


def attend_forward(queries, key_vecs, values, segment, score_scale):
    scores = masked_scores(queries, key_vecs, segment, score_scale)
    row_max = jnp.max(scores, axis=-1, keepdims=True)
    exp_scores = jnp.exp(scores - row_max)
    row_total = jnp.sum(exp_scores, axis=-1, keepdims=True)
    probs_low = to_low(exp_scores / row_total)
    attended = jnp.einsum("hlm,mhe->lhe", probs_low, values, preferred_element_type=jnp.float32)
    return (attended, (row_max + jnp.log(row_total))[..., 0])


def attend_backward(queries, key_vecs, values, output_low, grad_low, logsum, segment, score_scale):
    scores = masked_scores(queries, key_vecs, segment, score_scale)
    probs = jnp.exp(scores - logsum[..., None])
    grad_values = jnp.einsum(
        "hlm,lhe->mhe", to_low(probs), grad_low, preferred_element_type=jnp.float32
    )
    grad_probs = jnp.einsum("lhe,mhe->hlm", grad_low, values, preferred_element_type=jnp.float32)
    row_delta = jnp.sum(grad_low.astype(jnp.float32) * output_low.astype(jnp.float32), axis=-1)
    grad_scores = to_low(probs * (grad_probs - row_delta.T[:, :, None]) * score_scale)
    grad_queries = jnp.einsum(
        "hlm,mhe->lhe", grad_scores, key_vecs, preferred_element_type=jnp.float32
    )
    grad_keys = jnp.einsum("hlm,lhe->mhe", grad_scores, queries, preferred_element_type=jnp.float32)
    return (grad_queries, grad_keys, grad_values)


def newton_schulz(moment):
    iterate = to_low(moment * lax.rsqrt(jnp.sum(moment * moment) + STAT_EPS))
    for newton_step in range(5):
        gram = to_low(jnp.dot(iterate.T, iterate, preferred_element_type=jnp.float32))
        square = jnp.dot(gram, gram, preferred_element_type=jnp.float32)
        poly = to_low(NEWTON_B * gram.astype(jnp.float32) + NEWTON_C * square)
        iterate = to_low(
            NEWTON_A * iterate.astype(jnp.float32)
            + jnp.dot(iterate, poly, preferred_element_type=jnp.float32)
        )
    return iterate


def tile_blocks(qkv_block, out_block, up_block, down_block):
    tile_rows = qkv_block.shape[0]
    tile_cols = qkv_block.shape[2] // 2

    def split_cols(block_in):
        return block_in.reshape(
            block_in.shape[0], block_in.shape[1] // tile_cols, tile_cols
        ).transpose(1, 0, 2)

    down_part = down_block.reshape(
        down_block.shape[0] // tile_rows, tile_rows, down_block.shape[1] // tile_cols, tile_cols
    )
    down_part = down_part.transpose(0, 2, 1, 3).reshape(-1, tile_rows, tile_cols)
    return jnp.concatenate(
        [
            split_cols(qkv_block[:, 0]),
            split_cols(qkv_block[:, 1]),
            split_cols(qkv_block[:, 2]),
            split_cols(out_block),
            split_cols(up_block),
            down_part,
        ],
        axis=0,
    )


def body(
    inputs,
    cotangent,
    segments,
    positions,
    w_qkv,
    w_out,
    w_up,
    w_down,
    vectors,
    tile_moment,
    vector_moment,
):
    row_index = lax.axis_index("row")
    col_index = lax.axis_index("col")
    col_count = lax.axis_size("col")
    row_count_axis = lax.axis_size("row")
    local_rows, col_width = inputs.shape
    model_width = vectors.shape[1]
    row_width = w_qkv.shape[2]
    head_feats = row_width // col_count
    unit_width = w_up.shape[1] // col_count
    up_total = w_up.shape[1] * row_count_axis
    score_scale = HEAD_DIM ** (-0.5)
    feat_start = (row_index * col_count + col_index) * head_feats
    unit_start = (row_index * col_count + col_index) * unit_width
    col_start = col_index * col_width
    norm_gain = lax.dynamic_slice_in_dim(vectors[5], col_start, col_width)
    norm_shift = lax.dynamic_slice_in_dim(vectors[6], col_start, col_width)
    out_bias = lax.dynamic_slice_in_dim(vectors[3] + vectors[4], col_start, col_width)
    qkv_bias = lax.dynamic_slice_in_dim(vectors[0:3], feat_start, head_feats, axis=1)
    up_bias = lax.dynamic_slice_in_dim(vectors[7:].reshape(-1), unit_start, unit_width)
    x_val = inputs.astype(jnp.float32)
    row_stats = lax.psum((jnp.sum(x_val, axis=1), jnp.sum(x_val * x_val, axis=1)), "col")
    mean_x = (row_stats[0] / model_width)[:, None]
    var_x = (row_stats[1] / model_width)[:, None] - mean_x * mean_x
    inv_std = lax.rsqrt(var_x + NORM_EPS)
    x_hat = (x_val - mean_x) * inv_std
    normed = (x_hat * norm_gain + norm_shift).astype(jnp.bfloat16)
    gathered, cot_rows = (
        lax.all_gather(normed, "row", axis=0, tiled=True),
        lax.all_gather(cotangent, "row", axis=0, tiled=True),
    )
    seq_rows = gathered.shape[0]
    qkv_perm = (
        w_qkv.reshape(col_width, 3, col_count, head_feats)
        .transpose(0, 2, 1, 3)
        .reshape(col_width, col_count, 3 * head_feats)
    )
    w_in = jnp.concatenate([qkv_perm, w_up.reshape(col_width, col_count, unit_width)], axis=2)
    group_width = w_in.shape[2]
    w_in_flat = w_in.reshape(col_width, col_count * group_width)
    mixed_out = lax.psum_scatter(
        jnp.dot(gathered, w_in_flat, preferred_element_type=jnp.float32),
        "col",
        scatter_dimension=1,
        tiled=True,
    )
    qkv_part = mixed_out[:, : 3 * head_feats].reshape(seq_rows, 3, head_feats) + qkv_bias[None]
    up_pre = mixed_out[:, 3 * head_feats :] + up_bias
    heads_here = head_feats // HEAD_DIM
    seq_count = seq_rows // SEQ_LEN

    def by_seq(tensor_in):
        return tensor_in.reshape((seq_count, SEQ_LEN) + tensor_in.shape[1:])

    cosine, sine_tab = rotary_tables(positions)
    queries = rotate(
        qkv_part[:, 0].reshape(seq_rows, heads_here, HEAD_DIM), cosine, sine_tab, 1.0
    ).astype(jnp.bfloat16)
    key_vecs = rotate(
        qkv_part[:, 1].reshape(seq_rows, heads_here, HEAD_DIM), cosine, sine_tab, 1.0
    ).astype(jnp.bfloat16)
    values = qkv_part[:, 2].reshape(seq_rows, heads_here, HEAD_DIM).astype(jnp.bfloat16)
    attended, logsum = jax.vmap(attend_forward, in_axes=(0, 0, 0, 0, None))(
        by_seq(queries), by_seq(key_vecs), by_seq(values), by_seq(segments), score_scale
    )
    attn_low = attended.reshape(seq_rows, head_feats).astype(jnp.bfloat16)
    act_low = gelu_value(up_pre).astype(jnp.bfloat16)
    attn_rows, act_rows = (
        lax.all_gather(attn_low, "col", axis=1, tiled=True),
        lax.all_gather(act_low, "col", axis=1, tiled=True),
    )
    branch = lax.psum_scatter(
        jnp.dot(attn_rows, w_out, preferred_element_type=jnp.float32)
        + jnp.dot(act_rows, w_down, preferred_element_type=jnp.float32),
        "row",
        scatter_dimension=0,
        tiled=True,
    )
    result = x_val + branch + out_bias
    cot_val = cotangent.astype(jnp.float32)
    grad_w_out = jnp.einsum("ti,tj->ij", attn_rows, cot_rows, preferred_element_type=jnp.float32)
    grad_w_down = jnp.einsum("ti,tj->ij", act_rows, cot_rows, preferred_element_type=jnp.float32)
    back_attn = jnp.einsum("tj,ij->ti", cot_rows, w_out, preferred_element_type=jnp.float32)
    back_act = jnp.einsum("tj,ij->ti", cot_rows, w_down, preferred_element_type=jnp.float32)
    grad_attn, grad_act = (
        lax.psum_scatter(back_attn, "col", scatter_dimension=1, tiled=True),
        lax.psum_scatter(back_act, "col", scatter_dimension=1, tiled=True),
    )
    grad_attn_low = grad_attn.astype(jnp.bfloat16)
    grad_up = grad_act * gelu_slope(up_pre)
    g_queries, g_keys, g_values = jax.vmap(attend_backward, in_axes=(0, 0, 0, 0, 0, 0, 0, None))(
        by_seq(queries),
        by_seq(key_vecs),
        by_seq(values),
        by_seq(attn_low.reshape(seq_rows, heads_here, HEAD_DIM)),
        by_seq(grad_attn_low.reshape(seq_rows, heads_here, HEAD_DIM)),
        logsum,
        by_seq(segments),
        score_scale,
    )
    g_queries = rotate(
        g_queries.reshape(seq_rows, heads_here, HEAD_DIM), cosine, sine_tab, -1.0
    ).reshape(seq_rows, head_feats)
    g_keys = rotate(g_keys.reshape(seq_rows, heads_here, HEAD_DIM), cosine, sine_tab, -1.0).reshape(
        seq_rows, head_feats
    )
    g_values = g_values.reshape(seq_rows, head_feats)
    grad_mixed = jnp.concatenate([g_queries, g_keys, g_values, grad_up], axis=1)
    grad_cols = lax.all_gather(grad_mixed.astype(jnp.bfloat16), "col", axis=1, tiled=True)
    grad_w_in = jnp.einsum("ti,tj->ij", gathered, grad_cols, preferred_element_type=jnp.float32)
    grad_norm = lax.psum_scatter(
        jnp.einsum("tj,ij->ti", grad_cols, w_in_flat, preferred_element_type=jnp.float32),
        "row",
        scatter_dimension=0,
        tiled=True,
    )
    grad_hat = grad_norm * norm_gain
    back_stats = lax.psum((jnp.sum(grad_hat, axis=1), jnp.sum(grad_hat * x_hat, axis=1)), "col")
    grad_x = inv_std * (
        grad_hat
        - (back_stats[0] / model_width)[:, None]
        - x_hat * (back_stats[1] / model_width)[:, None]
    )
    grad_input = cot_val + grad_x
    qkv_sums = jnp.sum(grad_mixed[:, : 3 * head_feats].reshape(seq_rows, 3, head_feats), axis=0)
    out_sums = jnp.sum(cot_val, axis=0)
    norm_sums = jnp.stack(
        [out_sums, out_sums, jnp.sum(grad_norm * x_hat, axis=0), jnp.sum(grad_norm, axis=0)]
    )
    qkv_rows = lax.dynamic_update_slice_in_dim(
        jnp.zeros((3, model_width), jnp.float32), qkv_sums, feat_start, axis=1
    )
    norm_rows = lax.dynamic_update_slice_in_dim(
        jnp.zeros((4, model_width), jnp.float32), norm_sums, col_start, axis=1
    )
    up_rows = lax.dynamic_update_slice_in_dim(
        jnp.zeros((up_total,), jnp.float32), jnp.sum(grad_up, axis=0), unit_start, axis=0
    ).reshape(-1, model_width)
    local_vec = jnp.concatenate([qkv_rows, norm_rows, up_rows], axis=0)
    vec_grad = lax.psum(local_vec, ("dp", "row", "col"))
    scaled = vec_grad * lax.rsqrt(jnp.mean(vec_grad * vec_grad, axis=1, keepdims=True) + STAT_EPS)
    vec_moment_new = MOMENTUM_RATE * vector_moment + scaled
    vectors_new = vectors - VECTOR_RATE * vec_moment_new
    grad_perm = grad_w_in.reshape(col_width, col_count, group_width)
    grad_qkv = (
        grad_perm[:, :, : 3 * head_feats]
        .reshape(col_width, col_count, 3, head_feats)
        .transpose(0, 2, 1, 3)
        .reshape(col_width, 3, row_width)
    )
    grad_up_w = grad_perm[:, :, 3 * head_feats :].reshape(col_width, col_count * unit_width)
    grad_tiles = tile_blocks(grad_qkv, grad_w_out, grad_up_w, grad_w_down)
    owned_grads = lax.psum_scatter(grad_tiles[None, None], "dp", scatter_dimension=2, tiled=True)
    owned_count = owned_grads.shape[2]
    weight_tiles = lax.dynamic_slice_in_dim(
        tile_blocks(w_qkv, w_out, w_up, w_down), lax.axis_index("dp") * owned_count, owned_count, 0
    ).astype(jnp.float32)
    moment_new = MOMENTUM_RATE * tile_moment[0, 0] + owned_grads[0, 0]
    ortho_tiles = jax.vmap(newton_schulz)(moment_new)
    tile_ratio = math.sqrt(max(1.0, moment_new.shape[1] / moment_new.shape[2]))
    tiles_new = weight_tiles - MUON_RATE * tile_ratio * ortho_tiles.astype(jnp.float32)
    return (
        result,
        grad_input,
        owned_grads,
        tiles_new[None, None],
        moment_new[None, None],
        vec_grad,
        vectors_new,
        vec_moment_new,
    )


def solution(mesh):
    placed = (
        P(("dp", "row"), "col"),
        P(("dp", "row"), "col"),
        P("dp"),
        P("dp"),
        P("col", None, "row"),
        P("row", "col"),
        P("col", "row"),
        P("row", "col"),
        P(),
        P("row", "col", "dp", None, None),
        P(),
    )
    return jax.shard_map(
        body,
        mesh=mesh,
        in_specs=placed,
        out_specs=(
            P(("dp", "row"), "col"),
            P(("dp", "row"), "col"),
            P("row", "col", "dp", None, None),
            P("row", "col", "dp", None, None),
            P("row", "col", "dp", None, None),
            P(),
            P(),
            P(),
        ),
        check_vma=False,
    )
```

profile of v0, /device:TPU:0, one launch (start us, length us, event | category | flops | bytes accessed | tf_op | source)
XLA Modules:
  0.0 1773.4 jit_solution(18095130869114446671)
XLA Ops:
  9.2 13.5 all-reduce.1
  26.5 8.3 all-gather.12.cloned.1.call-done
  34.9 5.0 fusion.35
  59.6 16.2 fusion.33
  77.4 9.7 fusion.36
  91.7 47.6 %reduce-scatter.11.cloned.1.call-done = f32[2048,128]{1,0:T(8,128)} async-done(((f32[2048,512]{1,0:T(8,128)}), f32[2048,128]{1,0:T(8,128)}) %reduce-scatter.11.cloned.1.call-update) | async-done | bytes 1048592 | tf_op jit(solution)/shard_map/reduce_scatter | solution.py:239
  142.8 480.9 %reduce-scatter.7.cloned.1.call-done = f32[2048,896]{1,0:T(8,128)} async-done(((f32[2048,3584]{1,0:T(8,128)}), f32[2048,896]{1,0:T(8,128)}) %reduce-scatter.7.cloned.1.call-update) | async-done | bytes 7340048 | tf_op jit(solution)/shard_map/reduce_scatter | solution.py:194
  636.7 4.5 fusion.1
  645.8 4.0 multiply_reduce_fusion
  649.8 6.1 multiply_convert_fusion
  663.4 245.1 %reduce-scatter.13.cloned.1.call-done = f32[2048,512]{1,0:T(8,128)} async-done(((f32[2048,2048]{1,0:T(8,128)}), f32[2048,512]{1,0:T(8,128)}) %reduce-scatter.13.cloned.1.call-update) | async-done | bytes 4194320 | tf_op jit(solution)/shard_map/reduce_scatter | solution.py:240
  908.5 6.5 fusion.27
  920.4 250.0 %all-gather.14.cloned.1.call-done = bf16[2048,3584]{1,0:T(8,128)(2,1)} async-done(((bf16[2048,896]{1,0:T(8,128)(2,1)}), bf16[2048,3584]{1,0:T(8,128)(2,1)}) %all-gather.14.cloned.1.call-update) | async-done | bytes 14680080 | tf_op jit(solution)/shard_map/all_gather | solution.py:262
  1170.4 13.4 fusion.37
  1183.9 136.5 %all-gather.10.cloned.1.call-done = bf16[2048,2048]{1,0:T(8,128)(2,1)} async-done(((bf16[2048,512]{1,0:T(8,128)(2,1)}), bf16[2048,2048]{1,0:T(8,128)(2,1)}) %all-gather.10.cloned.1.call-update) | async-done | bytes 8388624 | tf_op jit(solution)/shard_map/all_gather | solution.py:223
  1320.3 10.5 fusion.34
  1330.9 35.5 %all-gather.8.cloned.1.call-done = bf16[2048,512]{0,1:T(8,128)(2,1)} async-done(((bf16[2048,128]{0,1:T(8,128)(2,1)}), bf16[2048,512]{0,1:T(8,128)(2,1)}) %all-gather.8.cloned.1.call-update) | async-done | bytes 2097168 | tf_op jit(solution)/shard_map/all_gather | solution.py:222
  1366.4 6.3 convolution_add_fusion
  1373.5 4.7 fusion.39
  1379.9 9.7 fusion.40
  1389.6 5.9 reshape.252
  1395.5 4.8 copy.120
  1400.2 11.4 fusion.38
  1420.9 5.7 copy.119
  1435.2 9.7 all-reduce
  1444.9 15.5 reduce-scatter.9.cloned.1.call-done
  1464.6 4.5 constant_dynamic-update-slice_fusion
  1471.2 4.0 copy.129
  1498.9 92.2 %all-reduce.4.cloned.1.call-done = f32[11,2048]{1,0:T(8,128)} async-done(((f32[11,2048]{1,0:T(8,128)}), f32[11,2048]{1,0:T(8,128)}) %all-reduce.4.cloned.1.call-update) | async-done | bytes 90128 | tf_op jit(solution)/shard_map/psum | solution.py:293
  1593.9 143.6 %reduce-scatter.17.cloned.1.call-done = f32[1,1,12,512,256]{4,3,2,1,0:T(8,128)} async-done(((f32[1,1,24,512,256]{4,3,2,1,0:T(8,128)}), f32[1,1,12,512,256]{4,3,2,1,0:T(8,128)}) %reduce-scatter.17.cloned.1.call-update) | async-done | bytes 6291472 | tf_op jit(solution)/shard_map/reduce_scatter | solution.py:306
  1737.4 5.7 fusion.2
  1759.9 5.5 subtract_bitcast_fusion
  (229 shorter events, 135.4 us)
Async XLA Ops:
  7.2 27.7 %all-gather.12.cloned.1.call-start = ((), (), s32[]{:S(2)}) async-start(), calls=%async_computation.11 | async-start | bytes 2621440 | tf_op jit(solution)/shard_map/all_gather | solution.py:183
  7.9 51.7 %all-gather.6.cloned.1.call-start = ((), (), s32[]{:S(2)}) async-start(), calls=%async_computation.6 | async-start | bytes 2621440 | tf_op jit(solution)/shard_map/all_gather | solution.py:182
  26.5 112.8 %reduce-scatter.11.cloned.1.call-start = ((), (), s32[]{:S(2)}) async-start(), calls=%async_computation.12 | async-start | bytes 5242880 | tf_op jit(solution)/shard_map/reduce_scatter | solution.py:239
  39.9 583.9 %reduce-scatter.7.cloned.1.call-start = ((), (), s32[]{:S(2)}) async-start(), calls=%async_computation.7 | async-start | bytes 36700160 | tf_op jit(solution)/shard_map/reduce_scatter | solution.py:194
  46.1 7.7 copy-start.3
  75.8 832.7 %reduce-scatter.13.cloned.1.call-start = ((), (), s32[]{:S(2)}) async-start(), calls=%async_computation.13 | async-start | bytes 20971520 | tf_op jit(solution)/shard_map/reduce_scatter | solution.py:240
  87.1 1083.3 %all-gather.14.cloned.1.call-start = ((), (), s32[]{:S(2)}) async-start(), calls=%async_computation.14 | async-start | bytes 18350080 | tf_op jit(solution)/shard_map/all_gather | solution.py:262
  633.3 3.4 copy-start
  636.7 4.5 copy-start.13
  645.8 4.1 copy-start.19
  649.8 6.1 copy-start.24
  660.1 248.4 %copy-start.35 = (f32[512]{0:T(512)S(1)}, f32[512]{0:T(512)}, u32[]{:S(2)}) copy-start(f32[512]{0:T(512)} %dynamic_slice.23) | copy-start | bytes 6148
  908.5 6.5 copy-start.15
  908.5 6.5 copy-start.16
  908.5 6.5 copy-start.17
  917.1 403.2 %all-gather.10.cloned.1.call-start = ((), (), s32[]{:S(2)}) async-start(), calls=%async_computation.9 | async-start | bytes 10485760 | tf_op jit(solution)/shard_map/all_gather | solution.py:223
  917.9 448.5 %all-gather.8.cloned.1.call-start = ((), (), s32[]{:S(2)}) async-start(), calls=%async_computation.8 | async-start | bytes 2621440 | tf_op jit(solution)/shard_map/all_gather | solution.py:222
  920.3 513.0 %reduce-scatter.15.cloned.1.call-start = ((), (), s32[]{:S(2)}) async-start(), calls=%async_computation.15 | async-start | bytes 5242880 | tf_op jit(solution)/shard_map/reduce_scatter | solution.py:264
  1183.8 276.6 %reduce-scatter.9.cloned.1.call-start = ((), (), s32[]{:S(2)}) async-start(), calls=%async_computation.10 | async-start | bytes 5242880 | tf_op jit(solution)/shard_map/reduce_scatter | solution.py:225
  1372.7 218.4 %all-reduce.4.cloned.1.call-start = ((), (), s32[]{:S(2)}) async-start(), calls=%async_computation.17 | async-start | bytes 262144 | tf_op jit(solution)/shard_map/psum | solution.py:293
  1373.5 6.4 copy-start.11
  1395.5 4.8 copy-start.38
  1427.6 3.1 copy-start.2
  1430.8 29.7 %copy-start.18 = (bf16[512,512]{1,0:T(8,128)(2,1)S(1)}, bf16[512,512]{1,0:T(8,128)(2,1)}, u32[]{:S(2)}) copy-start(bf16[512,512]{1,0:T(8,128)(2,1)} %param.12) | copy-start | bytes 1572868
  1464.5 272.9 %reduce-scatter.17.cloned.1.call-start = ((), (), s32[]{:S(2)}) async-start(), calls=%async_computation.16 | async-start | bytes 18874368 | tf_op jit(solution)/shard_map/reduce_scatter | solution.py:306
  1471.2 8.0 copy-start.4
  1480.3 5.7 copy-start.8
  1490.5 5.5 copy-start.7
  1496.0 96.2 %copy-start.27 = (f32[11,2048]{1,0:T(8,128)S(1)}, f32[11,2048]{1,0:T(8,128)}, u32[]{:S(2)}) copy-start(f32[11,2048]{1,0:T(8,128)} %param.19) | copy-start | bytes 270340
  1496.0 96.2 %copy-start.28 = (f32[11,2048]{1,0:T(8,128)S(1)}, f32[11,2048]{1,0:T(8,128)}, u32[]{:S(2)}) copy-start(f32[11,2048]{1,0:T(8,128)} %param.21) | copy-start | bytes 270340
  1743.1 2.7 copy-start.1
  1759.9 5.6 copy-start.20
  (20 other events, 31.7 us)
Sparse Core Ops, SparseCore 0:
  9.5 25.2 all-gather.11
  37.0 22.5 all-gather.5
  62.5 76.7 reduce-scatter.10
  141.5 482.1 reduce-scatter.6
  625.9 282.5 reduce-scatter.12
  917.3 253.0 all-gather.13
  1172.5 147.7 all-gather.9
  1322.5 43.8 all-gather.7
  1369.5 43.3 reduce-scatter.14
  1415.8 44.5 reduce-scatter.8
  1466.6 124.5 all-reduce.3
  1593.8 143.5 reduce-scatter.16
where the time goes:
time: 1780 us; the launch traced here: 1770 us
  waiting for transfers between devices  1460 us (82%)
  matrix products  116 us (7%)
  local copies, waits for them, and re-layouts  108 us (6%)
  other arithmetic  49.4 us (3%)
  blocking collectives  23.1 us (1%)
    reduce_scatter x1, waiting for transfers between devices, body(): lax.psum_scatter(jnp.dot(gathered, w_in_flat, preferred_element_type=jnp....  481 us
    all_gather x1, waiting for transfers between devices, body(): lax.all_gather(grad_mixed.astype(jnp.bfloat16), 'col', axis=1, tiled=True)  250 us
    reduce_scatter x1, waiting for transfers between devices, body(): lax.psum_scatter(back_act, 'col', scatter_dimension=1, tiled=True)  245 us
    reduce_scatter x1, waiting for transfers between devices, body(): lax.psum_scatter(grad_tiles[None, None], 'dp', scatter_dimension=2, tiled...  144 us
    all_gather x1, waiting for transfers between devices, body(): lax.all_gather(act_low, 'col', axis=1, tiled=True)  136 us
    psum x1, waiting for transfers between devices, body(): vec_grad = lax.psum(local_vec, ('dp', 'row', 'col'))  92.2 us
    reduce_scatter x1, waiting for transfers between devices, body(): lax.psum_scatter(back_attn, 'col', scatter_dimension=1, tiled=True)  47.6 us
  transfers between devices with their start and end apart: 12, of which 11 were waited for; matrix products, arithmetic and copies ran while one was open for 13% of the time, Pallas kernels for 0%

commit v1 on v0

--- a/solution.py
+++ b/solution.py
@@ -290,7 +290,7 @@
         jnp.zeros((up_total,), jnp.float32), jnp.sum(grad_up, axis=0), unit_start, axis=0
     ).reshape(-1, model_width)
     local_vec = jnp.concatenate([qkv_rows, norm_rows, up_rows], axis=0)
-    vec_grad = lax.psum(local_vec, ("dp", "row", "col"))
+    vec_grad = jnp.sum(lax.all_gather(local_vec, ("dp", "row", "col")), axis=0)
     scaled = vec_grad * lax.rsqrt(jnp.mean(vec_grad * vec_grad, axis=1, keepdims=True) + STAT_EPS)
     vec_moment_new = MOMENTUM_RATE * vector_moment + scaled
     vectors_new = vectors - VECTOR_RATE * vec_moment_new

time: 1780 us -> 1720 us (0.966)
  waiting for transfers between devices: 1460 us -> 1400 us
    psum x1 -> x0, waiting for transfers between devices: 92.2 us -> none  [body(): vec_grad = lax.psum(local_vec, ('dp', 'row', 'col'))]
    reduce_scatter x1, waiting for transfers between devices: 0.01 us -> 33.8 us  [body(): lax.psum_scatter(jnp.einsum('tj,ij->ti', grad_cols, w_in_flat, preferred_...]
    reduce_scatter x1, waiting for transfers between devices: 144 us -> 121 us  [body(): lax.psum_scatter(grad_tiles[None, None], 'dp', scatter_dimension=2, tiled...]
    reduce_scatter x1, waiting for transfers between devices: 15.5 us -> 34.1 us  [body(): lax.psum_scatter(jnp.dot(attn_rows, w_out, preferred_element_type=jnp.flo...]
    unnamed x101 -> x90, local copies, waits for them, and re-layouts: 34.4 us -> 35.7 us
  transfers between devices with their start and end apart: 12 -> 12, of which waited for: 11 -> 11; matrix products, arithmetic and copies ran while one was open for 13% -> 12% of each run, Pallas kernels for 0% -> 0%
where the time goes in v1:
time: 1720 us; the launch traced here: 1710 us
  waiting for transfers between devices  1400 us (81%)
  matrix products  115 us (7%)
  local copies, waits for them, and re-layouts  102 us (6%)
  other arithmetic  50.6 us (3%)
  blocking collectives  25.2 us (1%)
    reduce_scatter x1, waiting for transfers between devices, body(): lax.psum_scatter(jnp.dot(gathered, w_in_flat, preferred_element_type=jnp....  481 us
    all_gather x1, waiting for transfers between devices, body(): lax.all_gather(grad_mixed.astype(jnp.bfloat16), 'col', axis=1, tiled=True)  250 us
    reduce_scatter x1, waiting for transfers between devices, body(): lax.psum_scatter(back_act, 'col', scatter_dimension=1, tiled=True)  245 us
    all_gather x1, waiting for transfers between devices, body(): lax.all_gather(act_low, 'col', axis=1, tiled=True)  136 us
    reduce_scatter x1, waiting for transfers between devices, body(): lax.psum_scatter(grad_tiles[None, None], 'dp', scatter_dimension=2, tiled...  121 us
    reduce_scatter x1, waiting for transfers between devices, body(): lax.psum_scatter(back_attn, 'col', scatter_dimension=1, tiled=True)  48.1 us
    unnamed x90, local copies, waits for them, and re-layouts  35.7 us
    all_gather x1, waiting for transfers between devices, body(): lax.all_gather(attn_low, 'col', axis=1, tiled=True)  35.5 us
  transfers between devices with their start and end apart: 12, of which 11 were waited for; matrix products, arithmetic and copies ran while one was open for 12% of the time, Pallas kernels for 0%

profile of v1, /device:TPU:0, one launch (start us, length us, event | category | flops | bytes accessed | tf_op | source)
XLA Modules:
  0.0 1707.6 jit_solution(17378439827062314961)
XLA Ops:
  9.2 13.5 all-reduce.1
  26.5 8.3 all-gather.15.cloned.1.call-done
  34.9 5.0 fusion.35
  59.6 16.2 fusion.33
  77.4 9.7 fusion.36
  91.1 48.1 %reduce-scatter.11.cloned.1.call-done = f32[2048,128]{1,0:T(8,128)} async-done(((f32[2048,512]{1,0:T(8,128)}), f32[2048,128]{1,0:T(8,128)}) %reduce-scatter.11.cloned.1.call-update) | async-done | bytes 1048592 | tf_op jit(solution)/shard_map/reduce_scatter | solution.py:239
  142.8 480.9 %reduce-scatter.7.cloned.1.call-done = f32[2048,896]{1,0:T(8,128)} async-done(((f32[2048,3584]{1,0:T(8,128)}), f32[2048,896]{1,0:T(8,128)}) %reduce-scatter.7.cloned.1.call-update) | async-done | bytes 7340048 | tf_op jit(solution)/shard_map/reduce_scatter | solution.py:194
  636.7 4.5 fusion.1
  645.8 4.0 multiply_reduce_fusion
  649.8 6.0 multiply_convert_fusion
  663.3 245.2 %reduce-scatter.13.cloned.1.call-done = f32[2048,512]{1,0:T(8,128)} async-done(((f32[2048,2048]{1,0:T(8,128)}), f32[2048,512]{1,0:T(8,128)}) %reduce-scatter.13.cloned.1.call-update) | async-done | bytes 4194320 | tf_op jit(solution)/shard_map/reduce_scatter | solution.py:240
  908.5 6.5 fusion.27
  920.4 250.0 %all-gather.17.cloned.1.call-done = bf16[2048,3584]{1,0:T(8,128)(2,1)} async-done(((bf16[2048,896]{1,0:T(8,128)(2,1)}), bf16[2048,3584]{1,0:T(8,128)(2,1)}) %all-gather.17.cloned.1.call-update) | async-done | bytes 14680080 | tf_op jit(solution)/shard_map/all_gather | solution.py:262
  1170.4 13.4 fusion.37
  1183.8 136.5 %all-gather.13.cloned.1.call-done = bf16[2048,2048]{1,0:T(8,128)(2,1)} async-done(((bf16[2048,512]{1,0:T(8,128)(2,1)}), bf16[2048,2048]{1,0:T(8,128)(2,1)}) %all-gather.13.cloned.1.call-update) | async-done | bytes 8388624 | tf_op jit(solution)/shard_map/all_gather | solution.py:223
  1320.3 10.5 fusion.34
  1330.8 35.5 %all-gather.11.cloned.1.call-done = bf16[2048,512]{0,1:T(8,128)(2,1)} async-done(((bf16[2048,128]{0,1:T(8,128)(2,1)}), bf16[2048,512]{0,1:T(8,128)(2,1)}) %all-gather.11.cloned.1.call-update) | async-done | bytes 2097168 | tf_op jit(solution)/shard_map/all_gather | solution.py:222
  1366.4 6.3 convolution_add_fusion
  1379.1 33.8 %reduce-scatter.15.cloned.1.call-done = f32[512,512]{1,0:T(8,128)} async-done(((f32[2048,512]{1,0:T(8,128)}), f32[512,512]{1,0:T(8,128)}) %reduce-scatter.15.cloned.1.call-update) | async-done | bytes 1048592 | tf_op jit(solution)/shard_map/reduce_scatter | solution.py:264
  1414.7 11.7 all-reduce
  1426.4 34.1 %reduce-scatter.9.cloned.1.call-done = f32[512,512]{1,0:T(8,128)} async-done(((f32[2048,512]{1,0:T(8,128)}), f32[512,512]{1,0:T(8,128)}) %reduce-scatter.9.cloned.1.call-update) | async-done | bytes 1048592 | tf_op jit(solution)/shard_map/reduce_scatter | solution.py:225
  1464.6 9.9 fusion.40
  1474.5 5.9 reshape.252
  1480.4 4.8 copy.173
  1485.1 11.4 fusion.38
  1503.1 5.3 copy.172
  1514.0 4.5 copy-done.4
  1520.6 4.0 copy.182
  1524.6 4.2 reshape.256
  1551.8 120.6 %reduce-scatter.17.cloned.1.call-done = f32[1,1,12,512,256]{4,3,2,1,0:T(8,128)} async-done(((f32[1,1,24,512,256]{4,3,2,1,0:T(8,128)}), f32[1,1,12,512,256]{4,3,2,1,0:T(8,128)}) %reduce-scatter.17.cloned.1.call-update) | async-done | bytes 6291472 | tf_op jit(solution)/shard_map/reduce_scatter | solution.py:306
  1672.4 5.7 fusion.2
  1694.8 5.5 subtract_bitcast_fusion
  (219 shorter events, 130.7 us)
Async XLA Ops:
  7.2 27.7 %all-gather.15.cloned.1.call-start = ((), (), s32[]{:S(2)}) async-start(), calls=%async_computation.11 | async-start | bytes 2621440 | tf_op jit(solution)/shard_map/all_gather | solution.py:183
  7.9 51.7 %all-gather.9.cloned.1.call-start = ((), (), s32[]{:S(2)}) async-start(), calls=%async_computation.6 | async-start | bytes 2621440 | tf_op jit(solution)/shard_map/all_gather | solution.py:182
  26.5 112.8 %reduce-scatter.11.cloned.1.call-start = ((), (), s32[]{:S(2)}) async-start(), calls=%async_computation.12 | async-start | bytes 5242880 | tf_op jit(solution)/shard_map/reduce_scatter | solution.py:239
  39.9 583.9 %reduce-scatter.7.cloned.1.call-start = ((), (), s32[]{:S(2)}) async-start(), calls=%async_computation.7 | async-start | bytes 36700160 | tf_op jit(solution)/shard_map/reduce_scatter | solution.py:194
  46.1 7.7 copy-start.5
  75.8 832.7 %reduce-scatter.13.cloned.1.call-start = ((), (), s32[]{:S(2)}) async-start(), calls=%async_computation.13 | async-start | bytes 20971520 | tf_op jit(solution)/shard_map/reduce_scatter | solution.py:240
  87.1 1083.3 %all-gather.17.cloned.1.call-start = ((), (), s32[]{:S(2)}) async-start(), calls=%async_computation.14 | async-start | bytes 18350080 | tf_op jit(solution)/shard_map/all_gather | solution.py:262
  633.3 3.4 copy-start
  636.7 4.5 copy-start.15
  645.8 4.0 copy-start.21
  649.8 6.0 copy-start.26
  908.5 6.5 copy-start.17
  908.5 6.5 copy-start.18
  908.5 6.5 copy-start.19
  917.1 403.2 %all-gather.13.cloned.1.call-start = ((), (), s32[]{:S(2)}) async-start(), calls=%async_computation.9 | async-start | bytes 10485760 | tf_op jit(solution)/shard_map/all_gather | solution.py:223
  917.9 448.5 %all-gather.11.cloned.1.call-start = ((), (), s32[]{:S(2)}) async-start(), calls=%async_computation.8 | async-start | bytes 2621440 | tf_op jit(solution)/shard_map/all_gather | solution.py:222
  920.3 492.6 %reduce-scatter.15.cloned.1.call-start = ((), (), s32[]{:S(2)}) async-start(), calls=%async_computation.15 | async-start | bytes 5242880 | tf_op jit(solution)/shard_map/reduce_scatter | solution.py:264
  1183.8 276.6 %reduce-scatter.9.cloned.1.call-start = ((), (), s32[]{:S(2)}) async-start(), calls=%async_computation.10 | async-start | bytes 5242880 | tf_op jit(solution)/shard_map/reduce_scatter | solution.py:225
  1372.7 175.7 %all-gather.19.cloned.1.call-start = ((), (), s32[]{:S(2)}) async-start(), calls=%async_computation.17 | async-start | bytes 4325376 | tf_op jit(solution)/shard_map/all_gather | solution.py:293
  1374.0 38.9 %copy-start.11 = (bf16[512,512]{1,0:T(8,128)(2,1)S(1)}, bf16[512,512]{1,0:T(8,128)(2,1)}, u32[]{:S(2)}) copy-start(bf16[512,512]{1,0:T(8,128)(2,1)} %param.11) | copy-start | bytes 1572868
  1377.8 82.7 %copy-start.20 = (bf16[512,512]{1,0:T(8,128)(2,1)S(1)}, bf16[512,512]{1,0:T(8,128)(2,1)}, u32[]{:S(2)}) copy-start(bf16[512,512]{1,0:T(8,128)(2,1)} %param.12) | copy-start | bytes 1572868
  1379.1 85.5 %copy-start.13 = (bf16[2048,512]{1,0:T(8,128)(2,1)S(1)}, bf16[2048,512]{1,0:T(8,128)(2,1)}, u32[]{:S(2)}) copy-start(bf16[2048,512]{1,0:T(8,128)(2,1)} %all-gather.15.cloned.1.call-done) | copy-start | bytes 6291460
  1464.5 207.9 %reduce-scatter.17.cloned.1.call-start = ((), (), s32[]{:S(2)}) async-start(), calls=%async_computation.16 | async-start | bytes 18874368 | tf_op jit(solution)/shard_map/reduce_scatter | solution.py:306
  1480.3 4.8 copy-start.33
  1514.0 4.5 copy-start.4
  1520.6 8.2 copy-start.6
  1529.9 5.8 copy-start.10
  1539.9 5.5 copy-start.9
  1546.9 4.1 copy-start.29
  1546.9 4.1 copy-start.30
  1550.8 127.3 %copy-start.22 = (f32[11,2048]{1,0:T(8,128)}, f32[11,2048]{1,0:T(8,128)S(1)}, u32[]{:S(2)}) copy-start(f32[11,2048]{1,0:T(8,128)S(1)} %reduce_sum.141) | copy-start | bytes 270340
  1678.1 2.7 copy-start.1
  (15 other events, 23.1 us)
Sparse Core Ops, SparseCore 0:
  9.5 25.2 all-gather.14
  37.0 22.5 all-gather.8
  62.5 76.7 reduce-scatter.10
  141.5 482.1 reduce-scatter.6
  625.9 282.5 reduce-scatter.12
  917.3 253.0 all-gather.16
  1172.5 147.7 all-gather.12
  1322.5 43.8 all-gather.10
  1369.5 43.3 reduce-scatter.14
  1415.8 44.5 reduce-scatter.8
  1464.7 61.6 all-gather.18
  1529.0 143.3 reduce-scatter.16
